TPU v7x, 32 devices: a whole 2x2x4 slice. The times are simulated.
32 devices in a mesh: dp: 8 (over z, core), seq: 4 (over y, x).
Axes of the slice: x: 2, y: 2, z: 4, core: 2. Of those that a mesh axis runs over, the one named last changes fastest.
Arguments:
- layer_in: bfloat16 [8, 512, 2560], P('dp', 'seq'), may hold values from -6 to 6
- scan_in: bfloat16 [8, 512, 2560], P('dp', 'seq'), may hold values from -6 to 6
- step_size: float32 [8, 512, 40], P('dp', 'seq'), may hold values from 0.0024 to 0.041
- b_weight: bfloat16 [2560, 64], replicated, may hold values from -0.125 to 0.125
- c_weight: bfloat16 [2560, 64], replicated, may hold values from -0.125 to 0.125
- decay_rate: float32 [40], replicated, may hold values from 0.0005 to 10
- skip_gain: float32 [40], replicated, may hold values from 0.25 to 1.75
- out_grad: bfloat16 [8, 512, 2560], P('dp', 'seq'), may hold values from -6 to 6
- doc_lengths: int32 [8, 4], P('dp'), may hold values from 1 to 256, 512 in all within a row
- block_order: int32 [8, 4], P('dp'), may hold values from 0 to 3, each once within a row
Outputs:
- scan_out: bfloat16 [8, 512, 2560], P('dp', 'seq')
- b_weight_grad: float32 [2560, 64], replicated
- c_weight_grad: float32 [2560, 64], replicated
Inputs may be any that keep to these rules, and one draw needn't show every extreme that they name: `block_order`: each row holds 0 to 3 once each. `doc_lengths`: each row sums to 512; its longest document has 256 tokens.
All inputs are finite; a program needn't handle non-finite values.
Results may differ from a plain program's by a relative error of at most 0.0055.
Values sent between devices are 32-bit elements.
A program may use at most 128 MiB of HBM per device.

v0:
```python
import math

import jax
import jax.numpy as jnp
from jax import lax
from jax.sharding import PartitionSpec as P

precise = lax.Precision.HIGHEST


def link_weights(low_block, high_block, totals):
    block_count = totals.shape[0]
    places = jnp.arange(block_count, dtype=jnp.int32)
    inside = (low_block[:, None] < places[None, :]) & (places[None, :] < high_block[:, None])
    factors = jnp.where(inside[:, :, None], totals[None, :, :], jnp.float32(1.0))
    return jnp.prod(factors, axis=1) * (low_block < high_block).astype(jnp.float32)[:, None]


def per_device(
    layer_in,
    scan_in,
    step_size,
    b_weight,
    c_weight,
    decay_rate,
    skip_gain,
    out_grad,
    doc_lengths,
    block_order,
):
    row_count = scan_in.shape[1]
    head_count = decay_rate.shape[0]
    head_width = scan_in.shape[2] // head_count
    state_count = b_weight.shape[1]
    block_count = lax.axis_size("seq")
    group_count = lax.axis_size("dp")
    my_slot = lax.axis_index("seq")
    tokens = layer_in[0]
    b_mat = jnp.dot(tokens, b_weight, preferred_element_type=jnp.float32).astype(jnp.bfloat16)
    c_mat = jnp.dot(tokens, c_weight, preferred_element_type=jnp.float32).astype(jnp.bfloat16)
    b_float = b_mat.astype(jnp.float32)
    c_float = c_mat.astype(jnp.float32)
    order_row = block_order[0]
    my_block = lax.dynamic_index_in_dim(order_row, my_slot, 0, keepdims=False)
    lengths = doc_lengths[0]
    doc_ends = jnp.cumsum(lengths, dtype=jnp.int32)
    doc_starts = doc_ends - lengths
    positions = my_block * row_count + jnp.arange(row_count, dtype=jnp.int32)
    segment = jnp.sum((doc_starts[None, :] <= positions[:, None]).astype(jnp.int32), axis=1)
    begins = jnp.any(doc_starts[None, :] == positions[:, None], axis=1)
    step_sizes = step_size[0]
    log_rates = -step_sizes * decay_rate[None, :]
    offsets = jnp.arange(row_count, dtype=jnp.int32)
    lower_tri = offsets[:, None] >= offsets[None, :]
    cumlog = jnp.dot(lower_tri.astype(jnp.float32), log_rates, precision=precise)
    linked = (segment == segment[0]) & jnp.logical_not(begins[0])
    in_last = segment == segment[row_count - 1]
    entering = jnp.where(linked[:, None], jnp.exp(cumlog), jnp.float32(0.0))
    leaving = jnp.where(
        in_last[:, None], jnp.exp(cumlog[row_count - 1][None, :] - cumlog), jnp.float32(0.0)
    )
    block_total = entering[row_count - 1]
    x_heads = scan_in[0].reshape(row_count, head_count, head_width)
    grad_heads = out_grad[0].reshape(row_count, head_count, head_width)
    driven = x_heads.astype(jnp.float32) * step_sizes[:, :, None]
    pushed = driven * leaving[:, :, None]
    seen = grad_heads.astype(jnp.float32) * entering[:, :, None]
    own_state = jnp.einsum("thp,tn->hpn", pushed, b_float, precision=precise).reshape(
        head_count, head_width * state_count
    )
    own_adjoint = jnp.einsum("thp,tn->hpn", seen, c_float, precision=precise).reshape(
        head_count, head_width * state_count
    )
    all_totals = lax.all_gather(block_total[None, :], "seq", axis=0, tiled=True)
    held_slots = jnp.arange(block_count, dtype=jnp.int32)
    onehot = (order_row[None, :] == held_slots[:, None]).astype(jnp.float32)
    seq_totals = jnp.dot(onehot, all_totals, precision=precise)
    mine_vector = jnp.full((block_count,), my_block, jnp.int32)
    from_earlier = link_weights(order_row, mine_vector, seq_totals)
    from_later = link_weights(mine_vector, order_row, seq_totals)
    incoming = jnp.einsum(
        "ch,chz->hz",
        from_earlier,
        lax.all_gather(own_state[None], "seq", axis=0, tiled=True),
        precision=precise,
    )
    returning = jnp.einsum(
        "ch,chz->hz",
        from_later,
        lax.all_gather(own_adjoint[None], "seq", axis=0, tiled=True),
        precision=precise,
    )
    incoming = incoming.reshape(head_count, head_width, state_count)
    returning = returning.reshape(head_count, head_width, state_count)
    scores = jnp.einsum("tn,sn->ts", c_mat, b_mat, preferred_element_type=jnp.float32)
    causal = lower_tri & (segment[:, None] == segment[None, :])
    set_size = math.gcd(head_count, 16)
    set_count = head_count // set_size

    def per_set(set_index, totals_pair):
        out_acc, mix_acc = totals_pair
        head_first = set_index * set_size
        set_log = lax.dynamic_slice_in_dim(cumlog, head_first, set_size, 1)
        set_steps = lax.dynamic_slice_in_dim(step_sizes, head_first, set_size, 1)
        set_driven = lax.dynamic_slice_in_dim(driven, head_first, set_size, 1)
        set_inputs = lax.dynamic_slice_in_dim(x_heads, head_first, set_size, 1)
        set_cotan = lax.dynamic_slice_in_dim(grad_heads, head_first, set_size, 1)
        log_gaps = set_log.T[:, :, None] - set_log.T[:, None, :]
        decays = jnp.exp(jnp.where(causal[None], log_gaps, jnp.float32(-1e30)))
        mixed = decays * scores[None]
        y_part = jnp.einsum("hts,shp->thp", mixed, set_driven, precision=precise)
        intersect = jnp.einsum(
            "thp,shp->hts", set_cotan, set_inputs, preferred_element_type=jnp.float32
        )
        q_part = jnp.sum(decays * intersect * set_steps.T[:, None, :], axis=0)
        out_acc = lax.dynamic_update_slice_in_dim(out_acc, y_part, head_first, 1)
        return (out_acc, mix_acc + q_part)

    start_pair = (
        jnp.zeros((row_count, head_count, head_width), jnp.float32),
        jnp.zeros((row_count, row_count), jnp.float32),
    )
    y_intra, mixing = lax.fori_loop(0, set_count, per_set, start_pair)
    y_cross = jnp.einsum("tn,hpn->thp", c_float, incoming, precision=precise) * entering[:, :, None]
    y_total = y_intra + y_cross + skip_gain[None, :, None] * x_heads.astype(jnp.float32)
    scan_out = y_total.reshape(row_count, head_count * head_width).astype(jnp.bfloat16)[None]
    grad_c = jnp.dot(mixing, b_float, precision=precise) + jnp.einsum(
        "thp,hpn->tn", seen, incoming, precision=precise
    )
    grad_b = jnp.einsum("ts,tn->sn", mixing, c_float, precision=precise) + jnp.einsum(
        "thp,hpn->tn", pushed, returning, precision=precise
    )
    local_b = jnp.einsum(
        "td,tn->dn", tokens, grad_b.astype(jnp.bfloat16), preferred_element_type=jnp.float32
    )
    local_c = jnp.einsum(
        "td,tn->dn", tokens, grad_c.astype(jnp.bfloat16), preferred_element_type=jnp.float32
    )
    summed_b, summed_c = lax.psum((local_b, local_c), ("dp", "seq"))
    scale = 1.0 / (group_count * row_count * block_count)
    return (scan_out, summed_b * scale, summed_c * scale)


def solution(mesh):
    in_specs = (
        P("dp", "seq", None),
        P("dp", "seq", None),
        P("dp", "seq", None),
        P(),
        P(),
        P(),
        P(),
        P("dp", "seq", None),
        P("dp", None),
        P("dp", None),
    )
    out_specs = (P("dp", "seq", None), P(), P())
    return jax.shard_map(
        per_device, mesh=mesh, in_specs=in_specs, out_specs=out_specs, check_vma=False
    )
```

profile of v0, /device:TPU:0, one launch (start us, length us, event | category | flops | bytes accessed | tf_op | source)
XLA Modules:
  0.0 262.6 jit_solution(5989525888902868005)
XLA Ops:
  7.3 1.3 constant_dynamic-slice_fusion
  9.2 0.8 reduce-window_clone.1
  10.0 0.7 subtract_bitcast_fusion
  10.9 1.4 copy.37
  12.7 0.6 fusion.50
  13.4 0.3 convolution_convert_fusion
  13.7 1.3 broadcast_compare_fusion
  15.1 0.8 fusion.28
  16.0 1.3 broadcast_in_dim_reshape.6
  17.6 0.6 copy-done.7
  18.2 0.3 convolution_convert_fusion.1
  18.5 0.8 fusion.25
  19.3 1.3 broadcast_in_dim_reshape.7
  20.7 1.3 convert_multiply_fusion.1
  22.0 0.8 fusion.51
  23.0 0.6 iota_compare_fusion.8
  23.6 0.6 compare_convert_fusion
  24.2 1.2 bitcast_multiply_fusion.1
  25.4 1.2 bitcast_multiply_fusion
  26.6 9.7 %all-gather = f32[4,1,40]{2,1,0:T(1,128)S(1)} all-gather(f32[1,1,40]{2,1,0:T(1,128)S(1)} %bitcast.112), channel_id=1, replica_groups=mesh['dp'=8,'seq'=4] {'seq'}, dimensions={0}, use_global_device_ids=true | all-gather | bytes 800 | tf_op jit(solution)/shard_map/all_gather | solution.py:74
  37.1 13.5 %while.16 = (s32[]{:T(128)}, f32[128,40,64]{0,2,1:T(8,128)S(1)}, f32[128,128]{1,0:T(8,128)S(1)}, f32[128,40,64]{0,2,1:T(8,128)}, f32[128,40]{0,1:T(8,128)S(1)}, ...) while((s32[]{:T(128)}, f32[128,40,64]{0,2,1:T(8,128)S(1)}, ...), condition=%wide.region_4.5_spmd.clone, body=%wide.region_2.4_spmd.clone.sunk | while | flops 118554632 | bytes 1202889 | solution.py:123
  37.2 2.1 fusion.82
  39.4 0.3 fusion.83
  39.9 2.1 fusion.82
  42.0 0.3 fusion.83
  42.5 2.2 fusion.82
  44.7 0.3 fusion.83
  45.2 2.1 fusion.82
  47.4 0.3 fusion.83
  47.9 2.1 fusion.82
  50.0 0.3 fusion.83
  50.6 9.0 %all-gather.4.cloned.1.call-done = f32[4,40,4096]{2,1,0:T(8,128)} async-done(((f32[1,40,4096]{2,1,0:T(8,128)}), f32[4,40,4096]{2,1,0:T(8,128)}) %all-gather.4.cloned.1.call-update) | async-done | bytes 2621456 | tf_op jit(solution)/shard_map/all_gather | solution.py:84
  59.7 8.0 %fusion.20 = f32[40,1,4096]{2,1,0:T(1,128)S(1)} fusion(f32[4,40,1]{0,2,1:T(1,128)S(1)} %copy.44, f32[4,40,4096]{2,1,0:T(8,128)} %all-gather.4.cloned.1.call-done), kind=kOutput, calls=%fused_computation.28 | convolution fusion | flops 7864320 | bytes 3277440 | tf_op jit(solution)/shard_map/ch,chz->hz/dot_general | solution.py:81
  67.6 1.2 copy.59
  68.9 1.7 reshape.147
  70.5 31.1 %all-gather.6.cloned.1.call-done = f32[4,40,4096]{2,1,0:T(8,128)} async-done(((f32[1,40,4096]{2,1,0:T(8,128)}), f32[4,40,4096]{2,1,0:T(8,128)}) %all-gather.6.cloned.1.call-update) | async-done | bytes 2621456 | tf_op jit(solution)/shard_map/all_gather | solution.py:90
  101.6 8.2 %fusion.18 = f32[40,1,4096]{2,1,0:T(1,128)S(1)} fusion(f32[4,40,1]{0,2,1:T(1,128)S(1)} %copy.47, f32[4,40,4096]{2,1,0:T(8,128)} %all-gather.6.cloned.1.call-done), kind=kOutput, calls=%fused_computation.26 | convolution fusion | flops 7864320 | bytes 3277440 | tf_op jit(solution)/shard_map/ch,chz->hz/dot_general | solution.py:87
  109.8 0.4 copy.58
  110.2 1.6 reshape.148
  111.8 4.0 %convolution_bitcast_fusion.4 = f32[128,64]{0,1:T(8,128)S(1)} fusion(f32[128,40,64]{0,2,1:T(8,128)} %bitcast.101, f32[40,64,64]{2,1,0:T(8,128)} %reshape.148), kind=kOutput, calls=%fused_computation.47 | convolution fusion | flops 251658240 | bytes 1998848 | tf_op jit(solution)/shard_map/thp,hpn->tn/dot_general | solution.py:130
  116.0 1.1 convolution_bitcast_fusion.2
  117.1 2.3 convolution_bitcast_fusion.3
  119.7 1.1 convolution_bitcast_fusion.1
  120.8 2.2 fusion.24
  123.0 1.1 copy.43
  124.1 129.1 %all-reduce.3.cloned.1.call-done = (f32[2560,64]{0,1:T(8,128)}, f32[2560,64]{0,1:T(8,128)}) async-done(((f32[2560,64]{0,1:T(8,128)}, f32[2560,64]{0,1:T(8,128)}), (f32[2560,64]{0,1:T(8,128)}, f32[2560,64]{0,1:T(8,128)})) %all-reduce.3.cloned.1.call-update) | async-done | bytes 1310736 | tf_op jit(solution)/shard_map/psum | solution.py:139
  253.1 2.0 broadcast_multiply_fusion.1
  255.2 0.9 broadcast_multiply_fusion
  (61 shorter events, 3.1 us)
Async XLA Ops:
  7.2 6.2 %copy-start = (bf16[1,128,2560]{2,1,0:T(8,128)(2,1)S(1)}, bf16[1,128,2560]{2,1,0:T(8,128)(2,1)}, u32[]{:S(2)}) copy-start(bf16[1,128,2560]{2,1,0:T(8,128)(2,1)} %param.12) | copy-start | bytes 1966084
  7.2 5.1 %copy-start.5 = (f32[1,128,40]{1,2,0:T(8,128)S(1)}, f32[1,128,40]{1,2,0:T(8,128)}, u32[]{:S(2)}) copy-start(f32[1,128,40]{1,2,0:T(8,128)} %param.14) | copy-start | bytes 61444
  7.2 5.1 %copy-start.10 = (f32[40]{0:T(128)S(1)}, f32[40]{0:T(128)}, u32[]{:S(2)}) copy-start(f32[40]{0:T(128)} %param.17) | copy-start | bytes 484
  7.2 6.2 %copy-start.6 = (bf16[2560,64]{0,1:T(8,128)(2,1)S(1)}, bf16[2560,64]{0,1:T(8,128)(2,1)}, u32[]{:S(2)}) copy-start(bf16[2560,64]{0,1:T(8,128)(2,1)} %param.15) | copy-start | bytes 983044
  7.2 52.4 %all-gather.4.cloned.1.call-start = ((), (), s32[]{:S(2)}) async-start(), calls=%async_computation | async-start | bytes 3276800 | tf_op jit(solution)/shard_map/all_gather | solution.py:84
  15.9 1.4 copy-start.3
  17.2 1.0 copy-start.7
  17.3 84.4 %all-gather.6.cloned.1.call-start = ((), (), s32[]{:S(2)}) async-start(), calls=%async_computation.1 | async-start | bytes 3276800 | tf_op jit(solution)/shard_map/all_gather | solution.py:90
  20.6 3.0 %copy-start.8 = (s32[1,4]{1,0:T(1,128)S(1)}, s32[1,4]{1,0:T(1,128)}, u32[]{:S(2)}) copy-start(s32[1,4]{1,0:T(1,128)} %param.21) | copy-start | bytes 52
  20.6 232.5 %all-reduce.3.cloned.1.call-start = ((), (), s32[]{:S(2)}) async-start(), calls=%async_computation.2 | async-start | bytes 2621440 | tf_op jit(solution)/shard_map/psum | solution.py:139
  50.6 17.0 %copy-start.1 = (f32[128,40,64]{0,2,1:T(8,128)}, f32[128,40,64]{0,2,1:T(8,128)S(1)}, u32[]{:S(2)}) copy-start(f32[128,40,64]{0,2,1:T(8,128)S(1)} %get-tuple-element.173) | copy-start | bytes 3932164
  115.8 1.3 copy-start.2
  119.7 1.1 copy-start.9
  253.1 2.0 copy-start.4
Sparse Core Ops, SparseCore 0:
  17.4 42.2 all-gather.3
  62.1 39.5 all-gather.5
  120.9 132.1 all-reduce.2
where the time goes:
time: 263 us
  waiting for transfers between devices  169 us (64%)
  matrix products  43.1 us (16%)
  between operations  14.7 us (6%)
  local copies, waits for them, and re-layouts  13.5 us (5%)
  other arithmetic  11.7 us (4%)
  blocking collectives  9.7 us (4%)
    psum x1, waiting for transfers between devices, per_device(): summed_b, summed_c = lax.psum((local_b, local_c), ('dp', 'seq'))  129 us
    all_gather x1, waiting for transfers between devices, per_device(): lax.all_gather(own_adjoint[None], 'seq', axis=0, tiled=True)  31.1 us
    dot_general x5, matrix products, per_set(): y_part = jnp.einsum('hts,shp->thp', mixed, set_driven, precision=precise)  10.7 us
    all_gather x1, blocking collectives, per_device(): all_totals = lax.all_gather(block_total[None, :], 'seq', axis=0, tiled=True)  9.7 us
    all_gather x1, waiting for transfers between devices, per_device(): lax.all_gather(own_state[None], 'seq', axis=0, tiled=True)  9.04 us
    dot_general x1, matrix products, per_device(): jnp.einsum('ch,chz->hz', from_later, lax.all_gather(own_adjoint[None], 's...  8.21 us
    dot_general x1, matrix products, per_device(): jnp.einsum('ch,chz->hz', from_earlier, lax.all_gather(own_state[None], 's...  7.98 us
  transfers between devices with their start and end apart: 3, of which 3 were waited for; matrix products, arithmetic and copies ran while one was open for 14% of the time, Pallas kernels for 0%

commit v1 on v0

v1 whole, which is shorter than its diff:
```python
import functools
import math

import jax
import jax.numpy as jnp
from jax import lax
from jax.experimental import pallas as pl
from jax.experimental.pallas import tpu as pltpu
from jax.sharding import PartitionSpec as P

MESH = pl.DeviceIdType.MESH
F32 = jnp.float32
BF16 = jnp.bfloat16


def dot(a, b):
    return jnp.dot(a, b, preferred_element_type=F32)


def dot_nt(a, b):
    return lax.dot_general(a, b, (((1,), (1,)), ((), ())), preferred_element_type=F32)


def dot_tn(a, b):
    return lax.dot_general(a, b, (((0,), (0,)), ((), ())), preferred_element_type=F32)


def spread(values, expander):
    high = values.astype(BF16)
    low = (values - high.astype(F32)).astype(BF16)
    return dot(high, expander) + dot(low, expander)


def plan(n_dp, n_seq):
    cores = 2 if n_dp % 2 == 0 else 1
    nz = n_dp // cores
    nx = math.isqrt(n_seq)
    while n_seq % nx:
        nx -= 1
    return cores, nz, nx, n_seq // nx


def kernel(
    n_dp,
    n_seq,
    depth,
    tok_ref,
    x_ref,
    step_ref,
    bw_ref,
    cw_ref,
    rate_ref,
    skip_ref,
    g_ref,
    len_ref,
    order_ref,
    y_ref,
    grad_ref,
    u_buf,
    v_buf,
    ec_buf,
    yin_buf,
    t_send,
    t_recv,
    tot_send,
    tot_recv,
    part,
    whole,
    rs0,
    rs1,
    rs2,
    rs3,
    t_ssem,
    t_rsem,
    tot_ssem,
    tot_rsem,
    rs_ssem,
    rs_rsem,
    ag_ssem,
    ag_rsem,
):
    dp = lax.axis_index("dp")
    me = lax.axis_index("seq")
    cores, nz, nx, ny = plan(n_dp, n_seq)
    core, z = dp % cores, dp // cores
    px, py = me % nx, me // nx
    rows, inner = x_ref.shape[1], x_ref.shape[2]
    heads = step_ref.shape[2]
    width = inner // heads
    states = bw_ref.shape[1]
    cut = 512 if inner % 512 == 0 else inner

    def along_x(k):
        return (dp, py * nx + (px + k) % nx)

    def along_y(k):
        return (dp, ((py + k) % ny) * nx + px)

    def mixed(first, second, k):
        a, b = first(k)[1], second(k)[1]
        return (dp, (1 - core) * a + core * b)

    def to_core(k):
        return (z * cores + (core + k) % cores, me)

    def to_z(k):
        return (((z + k) % nz) * cores + core, me)

    if nx == ny and cores == 2:
        pos1, pos2 = (1 - core) * px + core * py, (1 - core) * py + core * px
        stage1 = functools.partial(mixed, along_x, along_y)
        stage2 = functools.partial(mixed, along_y, along_x)
    else:
        pos1, pos2, stage1, stage2 = px, py, along_x, along_y
    stages = (
        (cores, core, to_core, rs0),
        (nx, pos1, stage1, rs1),
        (ny, pos2, stage2, rs2),
        (nz, z, to_z, rs3),
    )

    barrier = pltpu.get_barrier_semaphore()
    greeted = 0
    for k in range(1, n_seq):
        pl.semaphore_signal(
            barrier, inc=1, device_id=(dp, (me + k) % n_seq), device_id_type=MESH
        )
        greeted += 1
    for count, _, peer, _ in (stages[0], stages[3]):
        for k in range(1, count):
            pl.semaphore_signal(barrier, inc=1, device_id=peer(k), device_id_type=MESH)
            greeted += 1

    mine = order_ref[0, me]
    first = mine * rows
    starts = []
    running = jnp.int32(0)
    for j in range(len_ref.shape[1]):
        starts.append(running)
        running = running + len_ref[0, j]

    def segment_of(place):
        total = jnp.zeros_like(place)
        for start in starts:
            total = total + jnp.where(place >= start, 1, 0)
        return total

    seg_col = segment_of(first + lax.broadcasted_iota(jnp.int32, (rows, 1), 0))
    seg_row = segment_of(first + lax.broadcasted_iota(jnp.int32, (1, rows), 1))
    begun = jnp.int32(0)
    first_seg = jnp.int32(0)
    last_seg = jnp.int32(0)
    for start in starts:
        begun = begun + jnp.where(start == first, 1, 0)
        first_seg = first_seg + jnp.where(start <= first, 1, 0)
        last_seg = last_seg + jnp.where(start <= first + rows - 1, 1, 0)
    link_seg = first_seg - 1000 * begun
    linked = jnp.where(seg_col == link_seg, F32(1.0), F32(0.0))
    in_last = jnp.where(seg_col == last_seg, F32(1.0), F32(0.0))
    through = jnp.where(
        jnp.full((1, heads), link_seg, jnp.int32) == last_seg, F32(1.0), F32(0.0)
    )

    spot_t = lax.broadcasted_iota(jnp.int32, (rows, rows), 0)
    spot_s = lax.broadcasted_iota(jnp.int32, (rows, rows), 1)
    lower = spot_t >= spot_s
    causal = lower & (seg_col == seg_row)
    steps = step_ref[0]
    cumlog = lax.dot_general(
        jnp.where(lower, F32(1.0), F32(0.0)),
        -(steps * rate_ref[...]),
        (((1,), (0,)), ((), ())),
        precision=lax.Precision.HIGHEST,
        preferred_element_type=F32,
    )
    grown = jnp.exp(cumlog)
    shrunk = jnp.exp(-cumlog) * steps
    total = grown[rows - 1 : rows, :] * through
    tot_send[...] = jnp.zeros_like(tot_send)
    tot_send[:, :heads] = jnp.broadcast_to(total, (tot_send.shape[0], heads))

    tokens = tok_ref[0]
    b_mat = dot(tokens, bw_ref[...]).astype(BF16)
    c_mat = dot(tokens, cw_ref[...]).astype(BF16)
    b_float, c_float = b_mat.astype(F32), c_mat.astype(F32)
    b_last = jnp.transpose(b_float * in_last).astype(BF16)
    c_linked = c_float * linked
    c_turned = jnp.transpose(c_linked).astype(BF16)
    c_linked = c_linked.astype(BF16)

    def expander(at):
        head = lax.broadcasted_iota(jnp.int32, (heads, cut), 0)
        lane = lax.broadcasted_iota(jnp.int32, (heads, cut), 1) + at
        inside = (lane >= head * width) & (lane < head * width + width)
        return jnp.where(inside, F32(1.0), F32(0.0)).astype(BF16)

    sent_orders = [order_ref[0, (me + k) % n_seq] for k in range(1, n_seq)]
    got_orders = [order_ref[0, (me + n_seq - k) % n_seq] for k in range(1, n_seq)]
    for at in range(0, inner, cut):
        lanes = slice(at, at + cut)
        spreader = expander(at)
        grown_x = spread(grown, spreader)
        ec_buf[:, lanes] = grown_x
        u_part = (x_ref[0, :, lanes].astype(F32) * spread(shrunk, spreader)).astype(BF16)
        v_part = (g_ref[0, :, lanes].astype(F32) * grown_x).astype(BF16)
        u_buf[:, lanes] = u_part
        v_buf[:, lanes] = v_part
        state = dot(b_last, u_part) * grown_x[rows - 1 : rows, :]
        adjoint = dot(c_turned, v_part)
        for k in range(1, n_seq):
            later = jnp.full(state.shape, sent_orders[k - 1], jnp.int32) > mine
            t_send[k - 1, :, lanes] = jnp.where(later, state, adjoint)

    pl.semaphore_wait(barrier, greeted)
    sends = []
    for k in range(1, n_seq):
        target = (dp, (me + k) % n_seq)
        for source, landing, ssem, rsem in (
            (tot_send, tot_recv.at[k - 1], tot_ssem, tot_rsem),
            (t_send.at[k - 1], t_recv.at[k - 1], t_ssem, t_rsem),
        ):
            copy = pltpu.make_async_remote_copy(
                src_ref=source,
                dst_ref=landing,
                send_sem=ssem.at[k - 1],
                recv_sem=rsem.at[k - 1],
                device_id=target,
                device_id_type=MESH,
            )
            copy.start()
            sends.append(copy)

    scores = jnp.where(causal, dot_nt(c_mat, b_mat), F32(0.0)).astype(BF16)
    mixing = jnp.zeros((rows, rows), F32)
    for at in range(0, inner, cut):
        lanes = slice(at, at + cut)
        u_part = u_buf[:, lanes]
        yin_buf[:, lanes] = dot(scores, u_part)
        mixing = mixing + dot_nt(v_buf[:, lanes], u_part)
    mixing = jnp.where(causal, mixing, F32(0.0))
    grad_c = dot(mixing.astype(BF16), b_mat)
    grad_b = dot(jnp.transpose(mixing).astype(BF16), c_mat)

    for copy in sends:
        copy.wait()

    weights = []
    for k in range(n_seq - 1):
        weight = jnp.ones((8, heads), F32)
        own = jnp.full((8, heads), got_orders[k], jnp.int32)
        low, high = jnp.minimum(own, mine), jnp.maximum(own, mine)
        for other in range(n_seq - 1):
            if other != k:
                inside = (low < got_orders[other]) & (got_orders[other] < high)
                weight = weight * jnp.where(inside, tot_recv[other, :, :heads], F32(1.0))
        weights.append(weight)
    skips = jnp.broadcast_to(skip_ref[...], (8, heads))
    cross_c = jnp.zeros((rows, states), F32)
    cross_b = jnp.zeros((rows, states), F32)
    for at in range(0, inner, cut):
        lanes = slice(at, at + cut)
        spreader = expander(at)
        incoming = jnp.zeros((states, cut), F32)
        returning = jnp.zeros((states, cut), F32)
        for k in range(n_seq - 1):
            term = t_recv[k, :, lanes] * spread(weights[k], spreader)[:1, :]
            earlier = jnp.full(term.shape, got_orders[k], jnp.int32) < mine
            incoming = incoming + jnp.where(earlier, term, F32(0.0))
            returning = returning + jnp.where(earlier, F32(0.0), term)
        grown_x = ec_buf[:, lanes]
        incoming = incoming.astype(BF16)
        returning = (returning * grown_x[rows - 1 : rows, :]).astype(BF16)
        y_part = grown_x * (yin_buf[:, lanes] + dot(c_linked, incoming))
        y_part = y_part + spread(skips, spreader)[:1, :] * x_ref[0, :, lanes].astype(F32)
        y_ref[0, :, lanes] = y_part.astype(BF16)
        cross_c = cross_c + dot_nt(v_buf[:, lanes], incoming)
        cross_b = cross_b + dot_nt(u_buf[:, lanes], returning)
    grad_c = (grad_c + cross_c * linked).astype(BF16)
    grad_b = (grad_b + cross_b * in_last).astype(BF16)

    part[:depth, :states] = dot_tn(tokens, grad_b)
    part[:depth, states:] = dot_tn(tokens, grad_c)
    if part.shape[0] > depth:
        part[depth:, :] = jnp.zeros((part.shape[0] - depth, part.shape[1]), F32)

    base = jnp.int32(0)
    extent = part.shape[0]
    owned = []
    used = 0
    for count, place, peer, landing in stages:
        extent = extent // count
        copies = []
        for k in range(1, count):
            theirs = pl.multiple_of(base + ((place + k) % count) * extent, 8)
            copy = pltpu.make_async_remote_copy(
                src_ref=part.at[pl.ds(theirs, extent)],
                dst_ref=landing.at[k - 1],
                send_sem=rs_ssem.at[used],
                recv_sem=rs_rsem.at[used],
                device_id=peer(k),
                device_id_type=MESH,
            )
            copy.start()
            copies.append(copy)
            used += 1
        base = pl.multiple_of(base + place * extent, 8)
        owned.append((base, extent))
        summed = part[pl.ds(base, extent), :]
        for k, copy in enumerate(copies):
            copy.wait()
            summed = summed + landing[k]
        part[pl.ds(base, extent), :] = summed
    whole[pl.ds(base, extent), :] = part[pl.ds(base, extent), :]

    used = 0
    for (count, place, peer, _), (at, extent) in zip(stages[::-1], owned[::-1]):
        copies = []
        for k in range(1, count):
            copy = pltpu.make_async_remote_copy(
                src_ref=whole.at[pl.ds(at, extent)],
                dst_ref=whole.at[pl.ds(at, extent)],
                send_sem=ag_ssem.at[used],
                recv_sem=ag_rsem.at[used],
                device_id=peer(k),
                device_id_type=MESH,
            )
            copy.start()
            copies.append(copy)
            used += 1
        for copy in copies:
            copy.wait()
    grad_ref[...] = whole[:depth, :]


def per_device(
    layer_in,
    scan_in,
    step_size,
    b_weight,
    c_weight,
    decay_rate,
    skip_gain,
    out_grad,
    doc_lengths,
    block_order,
):
    n_dp, n_seq = lax.axis_size("dp"), lax.axis_size("seq")
    rows, inner = scan_in.shape[1], scan_in.shape[2]
    depth, states = b_weight.shape
    cores, nz, nx, ny = plan(n_dp, n_seq)
    devices = n_dp * n_seq
    padded = devices * 8 * (-(-depth // (devices * 8)))
    landings = []
    extent = padded
    for count in (cores, nx, ny, nz):
        extent = extent // count
        landings.append(pltpu.VMEM((max(count - 1, 1), extent, 2 * states), F32))
    hops = max(cores + nx + ny + nz - 4, 1)
    links = max(n_seq - 1, 1)
    vmem = pl.BlockSpec(memory_space=pltpu.VMEM)
    smem = pl.BlockSpec(memory_space=pltpu.SMEM)
    dma = pltpu.SemaphoreType.DMA
    scan_out, grads = pl.pallas_call(
        functools.partial(kernel, n_dp, n_seq, depth),
        out_shape=(
            jax.ShapeDtypeStruct((1, rows, inner), BF16),
            jax.ShapeDtypeStruct((depth, 2 * states), F32),
        ),
        in_specs=[vmem] * 8 + [smem] * 2,
        out_specs=(vmem, vmem),
        scratch_shapes=[
            pltpu.VMEM((rows, inner), BF16),
            pltpu.VMEM((rows, inner), BF16),
            pltpu.VMEM((rows, inner), F32),
            pltpu.VMEM((rows, inner), F32),
            pltpu.VMEM((links, states, inner), F32),
            pltpu.VMEM((links, states, inner), F32),
            pltpu.VMEM((8, 128), F32),
            pltpu.VMEM((links, 8, 128), F32),
            pltpu.VMEM((padded, 2 * states), F32),
            pltpu.VMEM((padded, 2 * states), F32),
            *landings,
            dma((links,)),
            dma((links,)),
            dma((links,)),
            dma((links,)),
            dma((hops,)),
            dma((hops,)),
            dma((hops,)),
            dma((hops,)),
        ],
        compiler_params=pltpu.CompilerParams(
            collective_id=0, has_side_effects=True, vmem_limit_bytes=60 * 1024 * 1024
        ),
    )(
        layer_in,
        scan_in,
        step_size,
        b_weight,
        c_weight,
        decay_rate[None, :],
        skip_gain[None, :],
        out_grad,
        doc_lengths,
        block_order,
    )
    scale = 1.0 / (n_dp * n_seq * rows)
    return (scan_out, grads[:, :states] * scale, grads[:, states:] * scale)


def solution(mesh):
    blocks = P("dp", "seq", None)
    in_specs = (blocks, blocks, blocks, P(), P(), P(), P(), blocks, P("dp", None), P("dp", None))
    return jax.shard_map(
        per_device, mesh=mesh, in_specs=in_specs, out_specs=(blocks, P(), P()), check_vma=False
    )
```

time: 263 us -> 88.3 us (0.34)
  waiting for transfers between devices: 169 us -> 0 us
  Pallas kernels: 0 us -> 76.2 us
  matrix products: 43.1 us -> 0 us
  between operations: 14.7 us -> 0.65 us
  blocking collectives: 9.7 us -> 0 us
  other arithmetic: 11.7 us -> 2.24 us
  local copies, waits for them, and re-layouts: 13.5 us -> 8.85 us
    psum x1 -> x0, waiting for transfers between devices: 129 us -> none  [per_device(): summed_b, summed_c = lax.psum((local_b, local_c), ('dp', 'seq'))]
    pallas_call x0 -> x1, Pallas kernels: none -> 76.2 us  [per_device(): pl.pallas_call(functools.partial(kernel, n_dp, n_seq, depth), out_shape=(...]
    dot_general x26 -> x0, matrix products: 43.1 us -> none  [the longest x5 10.7 us: per_set(): y_part = jnp.einsum('hts,shp->thp', mixed, set_driven, precision=precise)]
    all_gather x2 -> x0, waiting for transfers between devices: 40.1 us -> none  [the longest x1 31.1 us: per_device(): lax.all_gather(own_adjoint[None], 'seq', axis=0, tiled=True)]
    all_gather x1 -> x0, blocking collectives: 9.7 us -> none  [per_device(): all_totals = lax.all_gather(block_total[None, :], 'seq', axis=0, tiled=True)]
    unnamed x25 -> x8, local copies, waits for them, and re-layouts: 3.48 us -> 8.85 us
    mul x7 -> x1, other arithmetic: 6.78 us -> 2.24 us  [per_device(): return (scan_out, grads[:, :states] * scale, grads[:, states:] * scale)]
    reshape x2 -> x0, local copies, waits for them, and re-layouts: 3.26 us -> none  [the longest x1 1.68 us: per_device(): incoming = incoming.reshape(head_count, head_width, state_count)]
  transfers between devices with their start and end apart: 3 -> 0, of which waited for: 3 -> 0; matrix products, arithmetic and copies ran while one was open for 14% -> 0% of each run, Pallas kernels for 0% -> 0%
where the time goes in v1:
time: 88.3 us; the launch traced here: 88 us
  Pallas kernels  76.2 us (86%)
  local copies, waits for them, and re-layouts  8.85 us (10%)
  other arithmetic  2.24 us (3%)
    pallas_call x1, Pallas kernels, per_device(): pl.pallas_call(functools.partial(kernel, n_dp, n_seq, depth), out_shape=(...  76.2 us
    unnamed x8, local copies, waits for them, and re-layouts  8.85 us
    mul x1, other arithmetic, per_device(): return (scan_out, grads[:, :states] * scale, grads[:, states:] * scale)  2.24 us

profile of v1, /device:TPU:0, one launch (start us, length us, event | category | flops | bytes accessed | tf_op | source)
XLA Modules:
  0.0 88.0 jit_solution(9442155046696273852)
XLA Ops:
  0.6 1.5 %copy.13.step_ref = f32[1,128,40]{2,1,0:T(8,128)} copy(f32[1,128,40]{1,2,0:T(8,128)} %param.12) | data formatting | bytes 40960 | tf_op args[2]
  2.1 2.1 %copy.14.bw_ref = bf16[2560,64]{1,0:T(8,128)(2,1)} copy(bf16[2560,64]{0,1:T(8,128)(2,1)} %param.13) | data formatting | bytes 655360 | tf_op args[3]
  4.1 2.1 %copy.15.cw_ref = bf16[2560,64]{1,0:T(8,128)(2,1)} copy(bf16[2560,64]{0,1:T(8,128)(2,1)} %param.14) | data formatting | bytes 655360 | tf_op args[4]
  6.2 76.2 %shard_map.121 = (bf16[1,128,2560]{2,1,0:T(8,128)(2,1)}, f32[2560,128]{1,0:T(8,128)}) custom-call(bf16[1,128,2560]{2,1,0:T(8,128)(2,1)} %tok_ref.1, bf16[1,128,2560]{2,1,0:T(8,128)(2,1)} %x_ref.1, f32[1,128,40]{2,1,0:T(8,128)} %copy.13.step_ref, bf16[2560,64]{1,0:T(8,128)(2,1)} %copy.14.bw_ref, bf16[2560,64]{1,0:T(8,128)(2,1)} %copy.15.cw_ref, ...), custom_call_target="tpu_custom_call" | custom-call | tf_op jit(solution)/shard_map/pallas_call | solution.py:363
  82.4 2.2 %slice_multiply_fusion = (f32[2560,64]{1,0:T(8,128)S(1)}, f32[2560,64]{1,0:T(8,128)S(1)}) fusion(f32[2560,128]{1,0:T(8,128)} %get-tuple-element.6), kind=kLoop, calls=%fused_computation | loop fusion | flops 327680 | bytes 2621440 | tf_op jit(solution)/shard_map/mul | solution.py:408
  84.7 1.2 %copy.17 = f32[2560,64]{0,1:T(8,128)} copy(f32[2560,64]{1,0:T(8,128)S(1)} %get-tuple-element.10) | data formatting | bytes 1310720
  85.9 0.0 copy-start
  85.9 1.2 %copy.16 = f32[2560,64]{0,1:T(8,128)} copy(f32[2560,64]{1,0:T(8,128)S(1)} %get-tuple-element.11) | data formatting | bytes 1310720
  87.1 0.0 copy-done
  87.1 0.8 copy.19
Async XLA Ops:
  85.9 1.2 %copy-start = (bf16[1,128,2560]{2,1,0:T(8,128)(2,1)S(1)}, bf16[1,128,2560]{2,1,0:T(8,128)(2,1)}, u32[]{:S(2)}) copy-start(bf16[1,128,2560]{2,1,0:T(8,128)(2,1)} %get-tuple-element.15) | copy-start | bytes 1966084

commit v2 on v1

--- a/solution.py
+++ b/solution.py
@@ -55,11 +55,13 @@
     len_ref,
     order_ref,
     y_ref,
-    grad_ref,
+    gb_ref,
+    gc_ref,
     u_buf,
     v_buf,
     ec_buf,
     yin_buf,
+    in_buf,
     t_send,
     t_recv,
     tot_send,
@@ -85,9 +87,10 @@
     core, z = dp % cores, dp // cores
     px, py = me % nx, me // nx
     rows, inner = x_ref.shape[1], x_ref.shape[2]
-    heads = step_ref.shape[2]
+    heads = step_ref.shape[1]
     width = inner // heads
-    states = bw_ref.shape[1]
+    states = bw_ref.shape[0]
+    lane_cut = 128
     cut = 512 if inner % 512 == 0 else inner
 
     def along_x(k):
@@ -155,8 +158,9 @@
         first_seg = first_seg + jnp.where(start <= first, 1, 0)
         last_seg = last_seg + jnp.where(start <= first + rows - 1, 1, 0)
     link_seg = first_seg - 1000 * begun
-    linked = jnp.where(seg_col == link_seg, F32(1.0), F32(0.0))
-    in_last = jnp.where(seg_col == last_seg, F32(1.0), F32(0.0))
+    linked = jnp.where(seg_row == link_seg, F32(1.0), F32(0.0))
+    in_last = jnp.where(seg_row == last_seg, F32(1.0), F32(0.0))
+    linked_col = jnp.where(seg_col == link_seg, F32(1.0), F32(0.0))
     through = jnp.where(
         jnp.full((1, heads), link_seg, jnp.int32) == last_seg, F32(1.0), F32(0.0)
     )
@@ -165,7 +169,7 @@
     spot_s = lax.broadcasted_iota(jnp.int32, (rows, rows), 1)
     lower = spot_t >= spot_s
     causal = lower & (seg_col == seg_row)
-    steps = step_ref[0]
+    steps = jnp.transpose(step_ref[0])
     cumlog = lax.dot_general(
         jnp.where(lower, F32(1.0), F32(0.0)),
         -(steps * rate_ref[...]),
@@ -180,13 +184,14 @@
     tot_send[:, :heads] = jnp.broadcast_to(total, (tot_send.shape[0], heads))
 
     tokens = tok_ref[0]
-    b_mat = dot(tokens, bw_ref[...]).astype(BF16)
-    c_mat = dot(tokens, cw_ref[...]).astype(BF16)
-    b_float, c_float = b_mat.astype(F32), c_mat.astype(F32)
-    b_last = jnp.transpose(b_float * in_last).astype(BF16)
-    c_linked = c_float * linked
-    c_turned = jnp.transpose(c_linked).astype(BF16)
-    c_linked = c_linked.astype(BF16)
+    both = jnp.concatenate([bw_ref[...], cw_ref[...]], axis=0)
+    rounded = dot_nt(tokens, both).astype(BF16)
+    turned = jnp.transpose(rounded.astype(F32))
+    b_mat, c_mat = rounded[:, :states], rounded[:, states:]
+    b_turned, c_turned = turned[:states, :], turned[states:, :]
+    b_last = (b_turned * in_last).astype(BF16)
+    c_open = (c_turned * linked).astype(BF16)
+    c_linked = (c_mat.astype(F32) * linked_col).astype(BF16)
 
     def expander(at):
         head = lax.broadcasted_iota(jnp.int32, (heads, cut), 0)
@@ -196,9 +201,29 @@
 
     sent_orders = [order_ref[0, (me + k) % n_seq] for k in range(1, n_seq)]
     got_orders = [order_ref[0, (me + n_seq - k) % n_seq] for k in range(1, n_seq)]
-    for at in range(0, inner, cut):
-        lanes = slice(at, at + cut)
-        spreader = expander(at)
+    pl.semaphore_wait(barrier, greeted)
+    pieces = inner // cut
+
+    def send(source, landing, ssem, rsem, k):
+        copy = pltpu.make_async_remote_copy(
+            src_ref=source,
+            dst_ref=landing,
+            send_sem=ssem,
+            recv_sem=rsem,
+            device_id=(dp, (me + k) % n_seq),
+            device_id_type=MESH,
+        )
+        copy.start()
+        return copy
+
+    tot_copies = [
+        send(tot_send, tot_recv.at[k - 1], tot_ssem.at[k - 1], tot_rsem.at[k - 1], k)
+        for k in range(1, n_seq)
+    ]
+    sends = []
+    for i in range(pieces):
+        lanes = slice(i * cut, i * cut + cut)
+        spreader = expander(i * cut)
         grown_x = spread(grown, spreader)
         ec_buf[:, lanes] = grown_x
         u_part = (x_ref[0, :, lanes].astype(F32) * spread(shrunk, spreader)).astype(BF16)
@@ -206,29 +231,22 @@
         u_buf[:, lanes] = u_part
         v_buf[:, lanes] = v_part
         state = dot(b_last, u_part) * grown_x[rows - 1 : rows, :]
-        adjoint = dot(c_turned, v_part)
+        adjoint = dot(c_open, v_part)
+        group = []
         for k in range(1, n_seq):
             later = jnp.full(state.shape, sent_orders[k - 1], jnp.int32) > mine
-            t_send[k - 1, :, lanes] = jnp.where(later, state, adjoint)
-
-    pl.semaphore_wait(barrier, greeted)
-    sends = []
-    for k in range(1, n_seq):
-        target = (dp, (me + k) % n_seq)
-        for source, landing, ssem, rsem in (
-            (tot_send, tot_recv.at[k - 1], tot_ssem, tot_rsem),
-            (t_send.at[k - 1], t_recv.at[k - 1], t_ssem, t_rsem),
-        ):
-            copy = pltpu.make_async_remote_copy(
-                src_ref=source,
-                dst_ref=landing,
-                send_sem=ssem.at[k - 1],
-                recv_sem=rsem.at[k - 1],
-                device_id=target,
-                device_id_type=MESH,
+            t_send[k - 1, i] = jnp.where(later, state, adjoint)
+            slot = (k - 1) * pieces + i
+            group.append(
+                send(
+                    t_send.at[k - 1, i],
+                    t_recv.at[k - 1, i],
+                    t_ssem.at[slot],
+                    t_rsem.at[slot],
+                    k,
+                )
             )
-            copy.start()
-            sends.append(copy)
+        sends.append(group)
 
     scores = jnp.where(causal, dot_nt(c_mat, b_mat), F32(0.0)).astype(BF16)
     mixing = jnp.zeros((rows, rows), F32)
@@ -238,10 +256,11 @@
         yin_buf[:, lanes] = dot(scores, u_part)
         mixing = mixing + dot_nt(v_buf[:, lanes], u_part)
     mixing = jnp.where(causal, mixing, F32(0.0))
-    grad_c = dot(mixing.astype(BF16), b_mat)
-    grad_b = dot(jnp.transpose(mixing).astype(BF16), c_mat)
-
-    for copy in sends:
+    mixing = mixing.astype(BF16)
+    grad_c = dot_nt(b_turned.astype(BF16), mixing)
+    grad_b = dot(c_turned.astype(BF16), mixing)
+
+    for copy in tot_copies:
         copy.wait()
 
     weights = []
@@ -255,34 +274,46 @@
                 weight = weight * jnp.where(inside, tot_recv[other, :, :heads], F32(1.0))
         weights.append(weight)
     skips = jnp.broadcast_to(skip_ref[...], (8, heads))
-    cross_c = jnp.zeros((rows, states), F32)
-    cross_b = jnp.zeros((rows, states), F32)
-    for at in range(0, inner, cut):
-        lanes = slice(at, at + cut)
-        spreader = expander(at)
+    cross_c = jnp.zeros((states, rows), F32)
+    cross_b = jnp.zeros((states, rows), F32)
+    for i in range(pieces):
+        lanes = slice(i * cut, i * cut + cut)
+        spreader = expander(i * cut)
+        factors = [spread(weight, spreader)[:1, :] for weight in weights]
         incoming = jnp.zeros((states, cut), F32)
         returning = jnp.zeros((states, cut), F32)
+        for copy in sends[i]:
+            copy.wait()
         for k in range(n_seq - 1):
-            term = t_recv[k, :, lanes] * spread(weights[k], spreader)[:1, :]
+            term = t_recv[k, i] * factors[k]
             earlier = jnp.full(term.shape, got_orders[k], jnp.int32) < mine
             incoming = incoming + jnp.where(earlier, term, F32(0.0))
             returning = returning + jnp.where(earlier, F32(0.0), term)
-        grown_x = ec_buf[:, lanes]
         incoming = incoming.astype(BF16)
-        returning = (returning * grown_x[rows - 1 : rows, :]).astype(BF16)
-        y_part = grown_x * (yin_buf[:, lanes] + dot(c_linked, incoming))
-        y_part = y_part + spread(skips, spreader)[:1, :] * x_ref[0, :, lanes].astype(F32)
-        y_ref[0, :, lanes] = y_part.astype(BF16)
-        cross_c = cross_c + dot_nt(v_buf[:, lanes], incoming)
-        cross_b = cross_b + dot_nt(u_buf[:, lanes], returning)
+        in_buf[:, lanes] = incoming
+        returning = (returning * ec_buf[rows - 1 : rows, lanes]).astype(BF16)
+        cross_c = cross_c + dot_nt(incoming, v_buf[:, lanes])
+        cross_b = cross_b + dot_nt(returning, u_buf[:, lanes])
     grad_c = (grad_c + cross_c * linked).astype(BF16)
     grad_b = (grad_b + cross_b * in_last).astype(BF16)
-
-    part[:depth, :states] = dot_tn(tokens, grad_b)
-    part[:depth, states:] = dot_tn(tokens, grad_c)
-    if part.shape[0] > depth:
-        part[depth:, :] = jnp.zeros((part.shape[0] - depth, part.shape[1]), F32)
-
+    grads = jnp.concatenate([grad_b, grad_c], axis=0)
+    share = 2 * states // 8
+    columns = depth // lane_cut
+    for i in range(columns):
+        block = dot(grads, tok_ref[0, :, i * lane_cut : (i + 1) * lane_cut])
+        part[i * share : (i + 1) * share] = block.reshape(share, 8, lane_cut)
+    for i in range(columns * share, part.shape[0]):
+        part[i] = jnp.zeros((8, lane_cut), F32)
+
+    def finish(i):
+        lanes = slice(i * cut, i * cut + cut)
+        y_part = yin_buf[:, lanes] + dot(c_linked, in_buf[:, lanes])
+        y_part = ec_buf[:, lanes] * y_part
+        skip_x = spread(skips, expander(i * cut))[:1, :]
+        y_part = y_part + skip_x * x_ref[0, :, lanes].astype(F32)
+        y_ref[0, :, lanes] = y_part.astype(BF16)
+
+    undone = list(range(pieces))
     base = jnp.int32(0)
     extent = part.shape[0]
     owned = []
@@ -291,7 +322,7 @@
         extent = extent // count
         copies = []
         for k in range(1, count):
-            theirs = pl.multiple_of(base + ((place + k) % count) * extent, 8)
+            theirs = base + ((place + k) % count) * extent
             copy = pltpu.make_async_remote_copy(
                 src_ref=part.at[pl.ds(theirs, extent)],
                 dst_ref=landing.at[k - 1],
@@ -303,14 +334,20 @@
             copy.start()
             copies.append(copy)
             used += 1
-        base = pl.multiple_of(base + place * extent, 8)
+        base = base + place * extent
         owned.append((base, extent))
-        summed = part[pl.ds(base, extent), :]
-        for k, copy in enumerate(copies):
+        for i in undone[:2]:
+            finish(i)
+        undone = undone[2:]
+        for copy in copies:
             copy.wait()
+        summed = part[pl.ds(base, extent)]
+        for k in range(len(copies)):
             summed = summed + landing[k]
-        part[pl.ds(base, extent), :] = summed
-    whole[pl.ds(base, extent), :] = part[pl.ds(base, extent), :]
+        part[pl.ds(base, extent)] = summed
+    whole[pl.ds(base, extent)] = part[pl.ds(base, extent)]
+    for i in undone:
+        finish(i)
 
     used = 0
     for (count, place, peer, _), (at, extent) in zip(stages[::-1], owned[::-1]):
@@ -329,7 +366,10 @@
             used += 1
         for copy in copies:
             copy.wait()
-    grad_ref[...] = whole[:depth, :]
+    for i in range(columns):
+        block = whole[i * share : (i + 1) * share].reshape(2 * states, lane_cut)
+        gb_ref[:, i * lane_cut : (i + 1) * lane_cut] = block[:states]
+        gc_ref[:, i * lane_cut : (i + 1) * lane_cut] = block[states:]
 
 
 def per_device(
@@ -349,39 +389,44 @@
     depth, states = b_weight.shape
     cores, nz, nx, ny = plan(n_dp, n_seq)
     devices = n_dp * n_seq
-    padded = devices * 8 * (-(-depth // (devices * 8)))
+    units = depth // 128 * (2 * states // 8)
+    padded = devices * (-(-units // devices))
     landings = []
     extent = padded
     for count in (cores, nx, ny, nz):
         extent = extent // count
-        landings.append(pltpu.VMEM((max(count - 1, 1), extent, 2 * states), F32))
+        landings.append(pltpu.VMEM((max(count - 1, 1), extent, 8, 128), F32))
     hops = max(cores + nx + ny + nz - 4, 1)
     links = max(n_seq - 1, 1)
+    cut = 512 if inner % 512 == 0 else inner
+    pieces = inner // cut
     vmem = pl.BlockSpec(memory_space=pltpu.VMEM)
     smem = pl.BlockSpec(memory_space=pltpu.SMEM)
     dma = pltpu.SemaphoreType.DMA
-    scan_out, grads = pl.pallas_call(
+    scan_out, b_sum, c_sum = pl.pallas_call(
         functools.partial(kernel, n_dp, n_seq, depth),
         out_shape=(
             jax.ShapeDtypeStruct((1, rows, inner), BF16),
-            jax.ShapeDtypeStruct((depth, 2 * states), F32),
+            jax.ShapeDtypeStruct((states, depth), F32),
+            jax.ShapeDtypeStruct((states, depth), F32),
         ),
         in_specs=[vmem] * 8 + [smem] * 2,
-        out_specs=(vmem, vmem),
+        out_specs=(vmem, vmem, vmem),
         scratch_shapes=[
             pltpu.VMEM((rows, inner), BF16),
             pltpu.VMEM((rows, inner), BF16),
             pltpu.VMEM((rows, inner), F32),
             pltpu.VMEM((rows, inner), F32),
-            pltpu.VMEM((links, states, inner), F32),
-            pltpu.VMEM((links, states, inner), F32),
+            pltpu.VMEM((states, inner), BF16),
+            pltpu.VMEM((links, pieces, states, cut), F32),
+            pltpu.VMEM((links, pieces, states, cut), F32),
             pltpu.VMEM((8, 128), F32),
             pltpu.VMEM((links, 8, 128), F32),
-            pltpu.VMEM((padded, 2 * states), F32),
-            pltpu.VMEM((padded, 2 * states), F32),
+            pltpu.VMEM((padded, 8, 128), F32),
+            pltpu.VMEM((padded, 8, 128), F32),
             *landings,
-            dma((links,)),
-            dma((links,)),
+            dma((links * pieces,)),
+            dma((links * pieces,)),
             dma((links,)),
             dma((links,)),
             dma((hops,)),
@@ -395,9 +440,9 @@
     )(
         layer_in,
         scan_in,
-        step_size,
-        b_weight,
-        c_weight,
+        jnp.swapaxes(step_size, 1, 2),
+        b_weight.T,
+        c_weight.T,
         decay_rate[None, :],
         skip_gain[None, :],
         out_grad,
@@ -405,7 +450,7 @@
         block_order,
     )
     scale = 1.0 / (n_dp * n_seq * rows)
-    return (scan_out, grads[:, :states] * scale, grads[:, states:] * scale)
+    return (scan_out, (b_sum * scale).T, (c_sum * scale).T)
 
 
 def solution(mesh):

time: 88.3 us -> 80.4 us (0.911)
  local copies, waits for them, and re-layouts: 8.85 us -> 0.84 us
    unnamed x8 -> x3, local copies, waits for them, and re-layouts: 8.85 us -> 0.84 us
    transpose x0 -> x1, other arithmetic: none -> 2.5 us  [per_device(): return (scan_out, (b_sum * scale).T, (c_sum * scale).T)]
    mul x1 -> x0, other arithmetic: 2.24 us -> none  [per_device(): return (scan_out, grads[:, :states] * scale, grads[:, states:] * scale)]
where the time goes in v2:
time: 80.4 us; the launch traced here: 80.2 us
  Pallas kernels  76.2 us (95%)
  other arithmetic  2.5 us (3%)
  local copies, waits for them, and re-layouts  0.84 us (1%)
    pallas_call x1, Pallas kernels, per_device(): pl.pallas_call(functools.partial(kernel, n_dp, n_seq, depth), out_shape=(...  76.2 us
    transpose x1, other arithmetic, per_device(): return (scan_out, (b_sum * scale).T, (c_sum * scale).T)  2.5 us

profile of v2, /device:TPU:0, one launch (start us, length us, event | category | flops | bytes accessed | tf_op | source)
XLA Modules:
  0.0 80.2 jit_solution(12641833526381392208)
XLA Ops:
  0.6 76.2 %shard_map.121 = (bf16[1,128,2560]{2,1,0:T(8,128)(2,1)}, f32[64,2560]{1,0:T(8,128)}, f32[64,2560]{1,0:T(8,128)}) custom-call(bf16[1,128,2560]{2,1,0:T(8,128)(2,1)} %tok_ref.1, bf16[1,128,2560]{2,1,0:T(8,128)(2,1)} %x_ref.1, f32[1,40,128]{2,1,0:T(8,128)} %bitcast.11, bf16[64,2560]{1,0:T(8,128)(2,1)} %bitcast.9, bf16[64,2560]{1,0:T(8,128)(2,1)} %bitcast.10, ...), custom_call_target="tpu_custom_call" | custom-call | tf_op jit(solution)/shard_map/pallas_call | solution.py:406
  76.8 0.0 copy-start
  76.9 2.5 %multiply_bitcast_fusion = (f32[2560,64]{0,1:T(8,128)}, f32[2560,64]{0,1:T(8,128)}) fusion(f32[64,2560]{1,0:T(8,128)} %get-tuple-element.8, f32[64,2560]{1,0:T(8,128)} %get-tuple-element.7), kind=kLoop, calls=%fused_computation | loop fusion | flops 327680 | bytes 2621440 | tf_op jit(solution)/shard_map/transpose | solution.py:453
  79.4 0.0 copy-done
  79.4 0.8 %copy.14 = bf16[1,128,2560]{2,1,0:T(8,128)(2,1)} copy(bf16[1,128,2560]{2,1,0:T(8,128)(2,1)S(1)} %copy-done) | data formatting | bytes 1310720
Async XLA Ops:
  76.8 2.5 %copy-start = (bf16[1,128,2560]{2,1,0:T(8,128)(2,1)S(1)}, bf16[1,128,2560]{2,1,0:T(8,128)(2,1)}, u32[]{:S(2)}) copy-start(bf16[1,128,2560]{2,1,0:T(8,128)(2,1)} %get-tuple-element.14) | copy-start | bytes 1966084
